TPU v7x, 32 devices: a whole 2x2x4 slice. The times are simulated.
32 devices in a mesh: slab: 4 (over y, core), patch: 8 (over z, x).
Axes of the slice: x: 2, y: 2, z: 4, core: 2. Of those that a mesh axis runs over, the one named last changes fastest.
Arguments:
- coarse: float32 [5, 64, 128, 128], P(None, 'slab', 'patch'), may hold values from -1.2 to 7.7, as said below
- fine: float32 [5, 128, 32, 1024], P(None, ('slab', 'patch')), may hold values from -1.2 to 7.7, as said below
- columns: int32 [32, 2], replicated, may hold values from 0 to 5, as said below
- patch_ids: int32 [4, 32], P('slab'), may hold values from 0 to 31, each once within a row
Outputs:
- coarse_out: float32 [5, 64, 128, 128], P(None, 'slab', 'patch')
- fine_out: float32 [5, 128, 32, 1024], P(None, ('slab', 'patch'))
Inputs may be any that keep to these rules, and one draw needn't show every extreme that they name: `coarse`: conserved variables of states with density and pressure between 0.5 and 2 and velocity components between -0.6 and 1.4. `fine`: conserved variables of states with density and pressure between 0.5 and 2 and velocity components between -0.6 and 1.4. `columns`: 32 distinct pairs (gy, gz) with gy below 6 and gz below 6. `patch_ids`: each row is a permutation of the 32 patch numbers of a slab.
All inputs are finite; a program needn't handle non-finite values.
Results may differ from a plain program's by a relative error of at most 0.00005.
Values sent between devices are 32-bit elements; how exact they have to be, the bound alone decides.
No kernel may reach another device: no remote copies, remote signals or barrier semaphores. Data moves between devices by JAX's collectives and lax.ppermute only.
A program may use at most 320 MiB of HBM per device.

v0:
```python
import jax
import jax.numpy as jnp
from jax import lax
from jax.sharding import PartitionSpec as P

P_SIZE = 32
LX = 1
GY = 6
GZ = 6
PYZ = 32
H = 16
heat_ratio = 1.4
fine_rate = 0.1
coarse_rate = 0.05
highest = lax.Precision.HIGHEST


def padded(block, sides, width):
    for axis, dim in sides:
        count = lax.axis_size(axis)
        forward = [(i, i + 1) for i in range(count - 1)]
        backward = [(target, source) for source, target in forward]
        low = lax.ppermute(
            lax.slice_in_dim(block, block.shape[dim] - width, None, axis=dim), axis, forward
        )
        high = lax.ppermute(lax.slice_in_dim(block, 0, width, axis=dim), axis, backward)
        block = jnp.concatenate([low, block, high], axis=dim)
    return block


def euler_flux(fields, normal_axis):
    density = fields[0]
    momentum = fields[1:4]
    energy = fields[4]
    velocity = momentum / density
    pressure = (heat_ratio - 1.0) * (energy - 0.5 * jnp.sum(momentum * velocity, axis=0))
    normal_speed = velocity[normal_axis]
    components = [
        momentum[normal_axis],
        momentum[0] * normal_speed,
        momentum[1] * normal_speed,
        momentum[2] * normal_speed,
        (energy + pressure) * normal_speed,
    ]
    components[1 + normal_axis] = components[1 + normal_axis] + pressure
    signal = jnp.abs(normal_speed) + jnp.sqrt(heat_ratio * pressure / density)
    return (jnp.stack(components), signal)


def rusanov(left_side, right_side, normal_axis):
    left_flux, left_signal = euler_flux(left_side, normal_axis)
    right_flux, right_signal = euler_flux(right_side, normal_axis)
    return 0.5 * (left_flux + right_flux) - 0.5 * jnp.maximum(left_signal, right_signal) * (
        right_side - left_side
    )


def advance(fields, ghosts):
    x_low, x_high, z_low, z_high, y_low, y_high = ghosts
    patch_count = fields.shape[1]
    side_cells = fields.shape[2]
    lane_count = side_cells * side_cells
    cube_view = fields.reshape(5, patch_count, side_cells, side_cells, side_cells)
    along_x = jnp.concatenate(
        [
            x_low.reshape(5, patch_count, 1, lane_count),
            fields,
            x_high.reshape(5, patch_count, 1, lane_count),
        ],
        axis=2,
    )
    flux_x = rusanov(along_x[:, :, :-1], along_x[:, :, 1:], 0)
    lane_index = jnp.arange(lane_count, dtype=jnp.int32)
    y_place = lane_index % side_cells
    z_place = lane_index // side_cells
    z_beyond = jnp.where(
        z_place == side_cells - 1,
        jnp.tile(z_high, (1, 1, 1, side_cells)),
        jnp.roll(fields, -side_cells, axis=3),
    )
    z_upper_flux = rusanov(fields, z_beyond, 2)
    z_edge = rusanov(z_low, cube_view[:, :, :, 0], 2)
    z_lower_flux = jnp.where(
        z_place == 0,
        jnp.tile(z_edge, (1, 1, 1, side_cells)),
        jnp.roll(z_upper_flux, side_cells, axis=3),
    )
    y_beyond = jnp.where(
        y_place == side_cells - 1,
        jnp.repeat(y_high, side_cells, axis=3),
        jnp.roll(fields, -1, axis=3),
    )
    y_upper_flux = rusanov(fields, y_beyond, 1)
    y_edge = rusanov(y_low, cube_view[..., 0], 1)
    y_lower_flux = jnp.where(
        y_place == 0, jnp.repeat(y_edge, side_cells, axis=3), jnp.roll(y_upper_flux, 1, axis=3)
    )
    change = (
        flux_x[:, :, 1:]
        - flux_x[:, :, :-1]
        + (z_upper_flux - z_lower_flux)
        + (y_upper_flux - y_lower_flux)
    )
    updated = fields - fine_rate * change
    y_top = y_upper_flux.reshape(5, patch_count, side_cells, side_cells, side_cells)[
        ..., side_cells - 1
    ]
    z_top = z_upper_flux[..., (side_cells - 1) * side_cells :]
    return (updated, (y_edge, y_top, z_edge, z_top))


def pair_mean(face_cells):
    extents = face_cells.shape
    return face_cells.reshape(extents[0], extents[1], extents[2] // 2, 2, extents[3] // 2, 2).mean(
        axis=(3, 5)
    )


def cell_mean(fields):
    extents = fields.shape
    return fields.reshape(
        extents[0], extents[1], extents[2] // 2, 2, extents[3] // 2, 2, extents[4] // 2, 2
    ).mean(axis=(3, 5, 7))


def upsample(face_cells):
    return jnp.repeat(jnp.repeat(face_cells, 2, axis=-2), 2, axis=-1)


def onehot(indices, extent):
    return (indices[:, None] == jnp.arange(extent, dtype=jnp.int32)[None, :]).astype(jnp.float32)


def neighbours(columns, step_y, step_z):
    matches = (columns[None, :, 0] == columns[:, None, 0] + step_y) & (
        columns[None, :, 1] == columns[:, None, 1] + step_z
    )
    present = jnp.any(matches, axis=1)
    partner = jnp.sum(
        jnp.where(matches, jnp.arange(columns.shape[0], dtype=jnp.int32)[None, :], 0), axis=1
    )
    return (present, partner)


def block_targets(column_y, column_z):
    grid_width = GY + 2
    return (
        (column_z + 1) * grid_width + column_y + 1,
        (column_z + 1) * grid_width + column_y,
        (column_z + 1) * grid_width + column_y + 2,
        column_z * grid_width + column_y + 1,
        (column_z + 2) * grid_width + column_y + 1,
    )


def cover_mask(columns):
    centre = block_targets(columns[:, 0], columns[:, 1])[0]
    occupied = jnp.sum(onehot(centre, (GZ + 2) * (GY + 2)), axis=0)
    return jnp.repeat(jnp.repeat(occupied.reshape(GZ + 2, GY + 2), H, axis=0), H, axis=1)


def block_form(slab):
    layer_depth = slab.shape[1] // H
    shaped = slab.reshape(5, layer_depth, H, GZ + 2, H, GY + 2, H).transpose(0, 1, 2, 4, 6, 3, 5)
    return shaped.reshape(5, layer_depth, H, H, H, (GZ + 2) * (GY + 2))


def slab_form(blocks):
    layer_depth = blocks.shape[1]
    shaped = blocks.reshape(5, layer_depth, H, H, H, GZ + 2, GY + 2).transpose(0, 1, 2, 5, 3, 6, 4)
    return shaped.reshape(5, layer_depth * H, (GZ + 2) * H, (GY + 2) * H)


def slot_order(numbers):
    slot_range = jnp.arange(numbers.shape[0], dtype=jnp.int32)
    found = jnp.sum(
        jnp.where(numbers[:, None] == slot_range[None, :], slot_range[:, None], 0), axis=0
    )
    return jnp.clip(found, 0, numbers.shape[0] - 1)


def coarse_faces(slab, layer_index, column_y, column_z):
    blocks = block_form(slab)
    layer_pick = onehot(layer_index, LX)
    centre, below_y, above_y, below_z, above_z = block_targets(column_y, column_z)
    nblocks = blocks.shape[-1]

    def select(portion, target):
        return jnp.einsum(
            "nl,nb,vlxzb->vnxz", layer_pick, onehot(target, nblocks), portion, precision=highest
        )

    return (
        select(blocks[:, :, :, :, H - 1], below_y),
        select(blocks[:, :, :, :, 0], above_y),
        select(blocks[:, :, :, H - 1], below_z),
        select(blocks[:, :, :, 0], above_z),
    )


def coarse_terms(averaged, face_terms, layer_index, column_y, column_z):
    layer_pick = onehot(layer_index, LX)
    centre, below_y, above_y, below_z, above_z = block_targets(column_y, column_z)
    nblocks = (GZ + 2) * (GY + 2)
    first_row = (jnp.arange(H) == 0).astype(jnp.float32)
    last_row = (jnp.arange(H) == H - 1).astype(jnp.float32)

    def spread(values, target):
        return jnp.einsum(
            "nl,nb,vnxz->vlxzb", layer_pick, onehot(target, nblocks), values, precision=highest
        )

    y_lower, y_upper, z_lower, z_upper = face_terms
    totals = jnp.einsum(
        "nl,nb,vnxzy->vlxzyb", layer_pick, onehot(centre, nblocks), averaged, precision=highest
    )
    totals = totals + spread(y_lower, below_y)[:, :, :, :, None, :] * last_row[:, None]
    totals = totals + spread(y_upper, above_y)[:, :, :, :, None, :] * first_row[:, None]
    totals = totals + spread(z_lower, below_z)[:, :, :, None, :, :] * last_row[:, None, None]
    totals = totals + spread(z_upper, above_z)[:, :, :, None, :, :] * first_row[:, None, None]
    return slab_form(totals)


def local(coarse, fine, columns, patch_ids):
    own_count = fine.shape[1]
    row_count = coarse.shape[2]
    patch_rank = lax.axis_index("patch")
    slab_rank = lax.axis_index("slab")
    slab_total = lax.axis_size("slab")
    numbers = patch_ids[0]
    own_numbers = lax.dynamic_slice_in_dim(numbers, patch_rank * own_count, own_count)
    inverse = slot_order(numbers)
    cube_fields = fine.reshape(5, own_count, P_SIZE, P_SIZE, P_SIZE)
    own_faces = jnp.stack(
        [
            cube_fields[:, :, 0],
            cube_fields[:, :, P_SIZE - 1],
            cube_fields[:, :, :, 0],
            cube_fields[:, :, :, P_SIZE - 1],
            cube_fields[..., 0],
            cube_fields[..., P_SIZE - 1],
        ]
    )
    slab_faces = lax.all_gather(own_faces, "patch", axis=2, tiled=True)
    slab_faces = jnp.take(slab_faces, inverse, axis=2)
    edge_faces = jnp.stack([slab_faces[0, :, :PYZ], slab_faces[1, :, -PYZ:]])
    rim_faces = padded(edge_faces, (("slab", 0),), 1)
    lower_rim = rim_faces[0]
    upper_rim = rim_faces[3]
    lower_source = jnp.where(slab_rank == 0, slab_faces[0, :, :PYZ], lower_rim)
    upper_source = jnp.where(slab_rank == slab_total - 1, slab_faces[1, :, -PYZ:], upper_rim)
    x_lower_table = jnp.concatenate([lower_source, slab_faces[1, :, :-PYZ]], axis=1)
    x_upper_table = jnp.concatenate([slab_faces[0, :, PYZ:], upper_source], axis=1)
    layer_index = own_numbers // PYZ
    column_index = own_numbers % PYZ
    column_y = columns[column_index, 0]
    column_z = columns[column_index, 1]
    whole_slab = lax.all_gather(coarse, "patch", axis=2, tiled=True)
    injected = coarse_faces(whole_slab, layer_index, column_y, column_z)

    def blend_faces(face_id, step_y, step_z, coarse_face):
        present, partner = neighbours(columns, step_y, step_z)
        target = layer_index * PYZ + partner[column_index]
        neighbour_face = jnp.take(slab_faces[face_id], target, axis=1)
        keep_mask = present[column_index][None, :, None, None]
        return jnp.where(keep_mask, neighbour_face, upsample(coarse_face))

    ghosts = (
        jnp.take(x_lower_table, own_numbers, axis=1),
        jnp.take(x_upper_table, own_numbers, axis=1),
        blend_faces(3, 0, -1, injected[2]),
        blend_faces(2, 0, 1, injected[3]),
        blend_faces(5, -1, 0, injected[0]),
        blend_faces(4, 1, 0, injected[1]),
    )
    updated, boundary = advance(fine, ghosts)

    def absent_mask(step_y, step_z):
        gaps = 1.0 - neighbours(columns, step_y, step_z)[0].astype(jnp.float32)
        return gaps[column_index][None, :, None, None]

    y_lower = -coarse_rate * pair_mean(boundary[0]) * absent_mask(-1, 0)
    y_upper = coarse_rate * pair_mean(boundary[1]) * absent_mask(1, 0)
    z_lower = -coarse_rate * pair_mean(boundary[2]) * absent_mask(0, -1)
    z_upper = coarse_rate * pair_mean(boundary[3]) * absent_mask(0, 1)
    averaged = cell_mean(updated.reshape(5, own_count, P_SIZE, P_SIZE, P_SIZE))
    placed = coarse_terms(
        averaged, (y_lower, y_upper, z_lower, z_upper), layer_index, column_y, column_z
    )
    contrib = lax.psum_scatter(placed, "patch", scatter_dimension=2, tiled=True)
    margin_cells = padded(coarse, (("slab", 1), ("patch", 2)), 1)
    before_x = jnp.where(slab_rank == 0, coarse[:, :1], margin_cells[:, :1, 1:-1])
    after_x = jnp.where(slab_rank == slab_total - 1, coarse[:, -1:], margin_cells[:, -1:, 1:-1])
    along_x = jnp.concatenate([before_x, coarse, after_x], axis=1)
    before_z = jnp.where(patch_rank == 0, coarse[:, :, :1], margin_cells[:, 1:-1, :1])
    after_z = jnp.where(
        patch_rank == lax.axis_size("patch") - 1, coarse[:, :, -1:], margin_cells[:, 1:-1, -1:]
    )
    along_z = jnp.concatenate([before_z, coarse, after_z], axis=2)
    along_y = jnp.concatenate([coarse[..., :1], coarse, coarse[..., -1:]], axis=3)
    covered = cover_mask(columns)
    own_cover = lax.dynamic_slice_in_dim(covered, patch_rank * row_count, row_count, 0)
    cover_z = lax.dynamic_slice_in_dim(
        jnp.pad(covered, ((1, 1), (0, 0))), patch_rank * row_count, row_count + 2, 0
    )
    cover_y = jnp.pad(own_cover, ((0, 0), (1, 1)))
    flux_x = rusanov(along_x[:, :-1], along_x[:, 1:], 0) * (1.0 - own_cover)
    flux_z = rusanov(along_z[:, :, :-1], along_z[:, :, 1:], 2) * (
        (1.0 - cover_z[:-1]) * (1.0 - cover_z[1:])
    )
    flux_y = rusanov(along_y[..., :-1], along_y[..., 1:], 1) * (
        (1.0 - cover_y[:, :-1]) * (1.0 - cover_y[:, 1:])
    )
    change = (
        flux_x[:, 1:]
        - flux_x[:, :-1]
        + (flux_z[:, :, 1:] - flux_z[:, :, :-1])
        + (flux_y[..., 1:] - flux_y[..., :-1])
    )
    provisional = coarse - coarse_rate * change
    coarse_out = jnp.where(own_cover > 0, contrib, provisional + contrib)
    return (coarse_out, updated)


def solution(mesh):
    return jax.shard_map(
        local,
        mesh=mesh,
        in_specs=(
            P(None, "slab", "patch", None),
            P(None, ("slab", "patch"), None, None),
            P(),
            P("slab", None),
        ),
        out_specs=(P(None, "slab", "patch", None), P(None, ("slab", "patch"), None, None)),
        check_vma=False,
    )
```

profile of v0, /device:TPU:0, one launch (start us, length us, event | category | flops | bytes accessed | tf_op | source)
XLA Modules:
  0.0 1050.5 jit_solution(5317102842722173065)
XLA Ops:
  7.2 7.9 reshape.643
  16.3 3.8 fusion.238
  20.1 16.2 %fusion.237 = (f32[5,4,32,32,1]{4,3,2,1,0:T(8,128)}, f32[5,4,32,32,1]{4,3,2,1,0:T(8,128)}) fusion(f32[5,4,32,32,32]{4,3,2,1,0:T(8,128)} %reshape.643), kind=kLoop, calls=%fused_computation.640 | loop fusion | bytes 327680 | tf_op jit(solution)/shard_map/slice | solution.py:241
  36.3 6.7 copy.483
  43.0 7.5 copy.484
  68.3 9.4 slice_reduce_fusion
  77.7 6.1 slice.909
  91.5 3.0 copy.502
  94.6 4.8 copy.501
  99.4 3.1 copy.503
  102.4 2.4 copy.499
  104.8 3.1 copy.500
  110.2 2.5 fusion.236
  127.0 145.6 %all-gather.3.cloned.1.call-done = f32[6,5,32,32,32]{4,3,1,2,0:T(8,128)} async-done(((f32[6,5,4,32,32]{4,3,1,2,0:T(8,128)}), f32[6,5,32,32,32]{4,3,1,2,0:T(8,128)}) %all-gather.3.cloned.1.call-update) | async-done | bytes 3932176 | tf_op jit(solution)/shard_map/all_gather | solution.py:244
  272.5 13.7 %gather_fusion.2 = f32[32,6,5,32,32]{4,3,2,1,0:T(8,128)} fusion(f32[6,5,32,32,32]{4,3,1,2,0:T(8,128)} %all-gather.3.cloned.1.call-done, s32[1024]{0:T(1024)S(1)} %pad_clamp_fusion.6), kind=kCustom, calls=%fused_computation.8 | custom fusion | bytes 7864448 | tf_op jit(solution)/shard_map/jit(_take)/gather | solution.py:245
  286.2 6.8 copy_bitcast_fusion.1
  303.7 8.2 select_bitcast_fusion.1
  311.8 3.1 gather_fusion.15
  315.0 3.1 gather_fusion.16
  325.2 3.1 gather_fusion.17
  330.6 3.1 gather_fusion.18
  333.7 3.1 gather_fusion.20
  341.5 18.0 %all-gather.5.cloned.1.call-done = f32[5,16,128,128]{3,2,1,0:T(8,128)} async-done(((f32[5,16,16,128]{3,2,1,0:T(8,128)}), f32[5,16,128,128]{3,2,1,0:T(8,128)}) %all-gather.5.cloned.1.call-update) | async-done | bytes 5242896 | tf_op jit(solution)/shard_map/all_gather | solution.py:258
  359.5 24.1 %reshape.646 = f32[5,1,16,8,16,8,16]{6,5,4,3,2,0,1:T(8,128)} reshape(f32[5,16,128,128]{3,2,1,0:T(8,128)} %all-gather.5.cloned.1.call-done) | data formatting | bytes 10485760 | tf_op jit(solution)/shard_map/reshape | solution.py:164
  383.6 29.2 %copy.537 = f32[5,1,16,8,16,8,16]{6,5,3,4,2,0,1:T(8,128)} copy(f32[5,1,16,8,16,8,16]{6,5,4,3,2,0,1:T(8,128)} %reshape.646) | data formatting | bytes 10485760 | tf_op jit(solution)/shard_map/reshape | solution.py:164
  412.8 56.7 %fusion.234 = (f32[5,1,16,16,1,64]{4,5,3,2,0,1:T(8,128)}, f32[5,1,16,16,1,64]{4,5,3,2,0,1:T(8,128)}) fusion(f32[5,1,16,16,16,64]{4,5,3,2,0,1:T(8,128)} %bitcast.634), kind=kLoop, calls=%fused_computation.637 | loop fusion | bytes 1310720 | tf_op jit(solution)/shard_map/slice | solution.py:194
  469.5 3.1 fusion.21
  477.0 23.0 %copy.496 = f32[5,1,16,16,1,64]{5,3,2,0,4,1:T(8,128)S(1)} copy(f32[5,1,16,16,1,64]{4,5,3,2,0,1:T(8,128)} %get-tuple-element.54) | data formatting | bytes 655360
  500.1 4.7 convolution_bitcast_fusion.4
  511.4 3.1 fusion.20
  515.4 4.7 tile.8
  520.0 9.0 tile.9
  529.0 22.6 %copy.495 = f32[5,1,16,16,1,64]{5,3,2,0,4,1:T(8,128)S(1)} copy(f32[5,1,16,16,1,64]{4,5,3,2,0,1:T(8,128)} %get-tuple-element.55) | data formatting | bytes 655360
  551.7 4.7 convolution_bitcast_fusion.5
  557.2 5.9 broadcast_in_dim.211
  563.1 9.3 reshape.657
  589.7 12.0 %constant_dynamic-update-slice_fusion.1 = (f32[5,4,33,1024]{3,2,1,0:T(8,128)}, f32[5,4,32,1024]{3,2,1,0:T(8,128)}, f32[5,4,32,1024]{3,2,1,0:T(8,128)}) fusion(f32[5,4,32,1024]{3,2,1,0:T(8,128)S(1)} %copy-done.2, f32[5,4,32,1024]{3,2,1,0:T(8,128)} %copy-done.6, f32[4,32,1024]{2,1,0:T(8,128)S(1)} %get-tuple-element.86, ...), kind=kLoop, calls=%fused_computation.344 | loop fusion | flops 6553599 | bytes 27262976
  601.7 8.1 reshape.663
  615.0 3.3 reduce_sum.257
  622.7 3.3 reduce_sum.256
  628.8 10.6 %slice.916 = f32[5,4,32,32,1]{4,3,2,1,0:T(8,128)} slice(f32[5,4,32,32,32]{4,3,2,1,0:T(8,128)} %reshape.663), slice={[0:5], [0:4], [0:32], [0:32], [31:32]} | slice | bytes 163840 | tf_op jit(solution)/shard_map/slice | solution.py:105
  639.4 27.1 %copy.504 = f32[5,4,32,32,1]{0,3,2,1,4:T(8,128)} copy(f32[5,4,32,32,1]{4,3,2,1,0:T(8,128)} %slice.916) | data formatting | bytes 163840
  666.5 3.3 reduce_sum.255
  672.7 3.3 reduce_sum.254
  678.8 3.0 dynamic-update-slice.79
  689.8 4.7 tile.20
  694.5 9.1 tile.21
  703.6 5.8 broadcast_in_dim.216
  709.4 9.1 reshape.661
  718.5 4.0 multiply_bitcast_fusion
  722.5 4.7 fusion.5
  728.5 3.9 fusion.11
  732.4 34.2 %copy.452 = f32[5,4,32,1024]{0,3,2,1:T(8,128)} copy(f32[5,4,32,1024]{3,2,1,0:T(8,128)} %fusion.11) | data formatting | bytes 5242880 | tf_op jit(solution)/shard_map/sub | solution.py:104
  766.6 49.4 %reduce_sum.253 = f32[5,4,16,16,16]{0,4,3,2,1:T(8,128)} reduce(f32[5,4,16,2,16,2,16,2]{0,7,6,5,4,3,2,1:T(2,128)} %bitcast.120, f32[]{:T(128)} %constant.88.clone.1), dimensions={3,5,7}, to_apply=%region_19.21 | reduce | flops 573440 | bytes 2949124 | tf_op jit(solution)/shard_map/reduce_sum | solution.py:123
  816.0 9.3 copy.453
  827.1 23.2 %fusion.2 = f32[5,1,16,16,16,64]{5,4,3,2,0,1:T(8,128)} fusion(f32[16]{0:T(128)S(1)} %copy-done.77, f32[5,16,16,64]{3,2,1,0:T(8,128)S(1)} %copy-done.46, f32[16]{0:T(128)S(1)} %copy-done.78, f32[5,16,16,64]{3,2,1,0:T(8,128)S(1)} %copy-done.47, f32[5,16,16,64]{3,2,1,0:T(8,128)S(1)} %copy-done.48, f32[5,16,16,64]{3,2,1,0:T(8,128)S(1)} %copy-done.49, ...), kind=kOutput, calls=%fused_computation.33 | convolution fusion | flops 73400832 | bytes 6881440 | tf_op jit(solution)/shard_map/nl,nb,vnxzy->vlxzyb/dot_general | solution.py:214
  850.2 24.4 %copy.467 = f32[5,1,16,16,16,64]{4,5,3,2,0,1:T(8,128)} copy(f32[5,1,16,16,16,64]{5,4,3,2,0,1:T(8,128)} %fusion.2) | data formatting | bytes 10485760 | tf_op jit(solution)/shard_map/add | solution.py:220
  874.6 29.1 %copy.468 = f32[5,1,16,8,16,8,16]{6,5,4,3,2,0,1:T(8,128)} copy(f32[5,1,16,8,16,8,16]{6,5,3,4,2,0,1:T(8,128)} %bitcast.637) | data formatting | bytes 10485760 | tf_op jit(solution)/shard_map/transpose | solution.py:170
  903.7 26.5 %reshape.667 = f32[5,16,128,128]{3,2,1,0:T(8,128)} reshape(f32[5,1,16,8,16,8,16]{6,5,4,3,2,0,1:T(8,128)} %copy.468) | data formatting | bytes 10485760 | tf_op jit(solution)/shard_map/reshape | solution.py:171
  931.2 11.1 %collective-permute-start.2 = (f32[5,1,16,128]{3,2,1,0:T(8,128)S(1)}, f32[5,1,16,128]{3,2,1,0:T(8,128)S(1)}, u32[]{:S(2)}, u32[]{:S(2)}) collective-permute-start(f32[5,1,16,128]{3,2,1,0:T(8,128)S(1)} %get-tuple-element.142), channel_id=1, source_target_pairs={{0,8},{8,16},{16,24},{1,9},{9,17},{17,25},{2,10},{10,18},{18,26},{... | collective-permute-start | bytes 122888 | tf_op jit(solution)/shard_map/ppermute | solution.py:23
  948.2 2.5 collective-permute-start.4
  952.8 4.3 collective-permute-done.5
  958.4 82.4 %reduce-scatter.2.cloned.1.call-done = f32[5,16,16,128]{3,2,1,0:T(8,128)} async-done(((f32[5,16,128,128]{3,2,1,0:T(8,128)}), f32[5,16,16,128]{3,2,1,0:T(8,128)}) %reduce-scatter.2.cloned.1.call-update) | async-done | bytes 655376 | tf_op jit(solution)/shard_map/reduce_scatter | solution.py:290
  1040.8 2.9 add_select_fusion
  (378 shorter events, 136.1 us)
Async XLA Ops:
  7.2 265.3 %all-gather.3.cloned.1.call-start = ((), (), s32[]{:S(2)}) async-start(), calls=%async_computation.1 | async-start | bytes 17694720 | tf_op jit(solution)/shard_map/all_gather | solution.py:244
  43.0 10.7 %copy-start.30 = (f32[5,4,32,32,1]{3,2,0,1,4:T(8,128)}, f32[5,4,32,32,1]{3,2,0,1,4:T(8,128)S(1)}, u32[]{:S(2)}) copy-start(f32[5,4,32,32,1]{3,2,0,1,4:T(8,128)S(1)} %copy.483) | copy-start | bytes 245764
  50.4 3.9 copy-start.42
  50.5 6.2 copy-start
  51.8 6.0 copy-start.1
  55.2 304.4 %all-gather.5.cloned.1.call-start = ((), (), s32[]{:S(2)}) async-start(), calls=%async_computation.2 | async-start | bytes 5898240 | tf_op jit(solution)/shard_map/all_gather | solution.py:258
  55.9 984.9 %reduce-scatter.2.cloned.1.call-start = ((), (), s32[]{:S(2)}) async-start(), calls=%async_computation.3 | async-start | bytes 5898240 | tf_op jit(solution)/shard_map/reduce_scatter | solution.py:290
  60.0 2.2 copy-start.65
  112.8 13.0 %copy-start.52 = (f32[1,4,32,1,32]{4,3,2,1,0:T(1,128)}, f32[1,4,32,1,32]{4,3,2,1,0:T(1,128)S(1)}, u32[]{:S(2)}) copy-start(f32[1,4,32,1,32]{4,3,2,1,0:T(1,128)S(1)} %get-tuple-element.70) | copy-start | bytes 49156
  120.2 4.1 copy-start.58
  121.2 3.1 copy-start.45
  121.2 165.0 %copy-start.56 = (f32[4,32,32]{2,1,0:T(8,128)}, f32[4,32,32]{2,1,0:T(8,128)S(1)}, u32[]{:S(2)}) copy-start(f32[4,32,32]{2,1,0:T(8,128)S(1)} %get-tuple-element.161) | copy-start | bytes 49156
  293.0 4.2 copy-start.35
  293.7 6.7 collective-permute-start
  295.1 8.5 collective-permute-start.1
  325.2 15.4 %copy-start.22 = (f32[5,4,1,1024]{3,2,1,0:T(1,128)}, f32[5,4,1,1024]{3,2,1,0:T(1,128)S(1)}, u32[]{:S(2)}) copy-start(f32[5,4,1,1024]{3,2,1,0:T(1,128)S(1)} %copy.387) | copy-start | bytes 245764
  338.2 2.3 copy-start.13
  338.2 2.3 copy-start.19
  469.5 3.8 copy-start.38
  500.1 5.4 copy-start.37
  500.1 5.4 copy-start.68
  504.8 2.5 copy-start.31
  511.4 3.8 copy-start.36
  511.4 3.8 copy-start.67
  529.0 22.7 %copy-start.63 = (s32[4]{0:T(128)S(1)}, s32[4]{0:T(128)}, u32[]{:S(2)}) copy-start(s32[4]{0:T(128)} %broadcast_add_fusion) | copy-start | bytes 52
  551.7 5.4 copy-start.64
  551.7 5.4 copy-start.66
  563.1 9.3 slice-start.1
  563.1 9.4 copy-start.15
  563.1 9.4 copy-start.70
  574.9 2.6 copy-start.24
  575.3 2.9 copy-start.2
  575.3 3.4 copy-start.11
  575.3 3.5 copy-start.34
  580.6 3.6 copy-start.26
  580.6 2.8 copy-start.14
  580.6 2.8 copy-start.69
  587.3 2.5 copy-start.27
  612.7 6.8 copy-start.28
  612.8 6.8 copy-start.74
  618.4 8.2 copy-start.73
  666.5 3.9 copy-start.72
  669.9 6.7 copy-start.71
  670.5 8.2 copy-start.60
  684.0 2.5 copy-start.4
  686.2 2.7 copy-start.12
  686.2 2.7 copy-start.21
  694.5 9.1 copy-start.40
  709.4 9.1 copy-start.20
  709.4 9.1 copy-start.23
  718.5 4.0 copy-start.5
  722.4 4.8 copy-start.8
  722.4 4.8 copy-start.9
  722.5 5.2 copy-start.17
  722.5 6.0 copy-start.18
  722.5 6.0 copy-start.29
  722.5 6.0 copy-start.41
  722.5 6.0 copy-start.61
  722.5 6.0 copy-start.62
  930.2 13.5 %copy-start.75 = (s32[32]{0:T(128)S(1)}, s32[32]{0:T(128)}, u32[]{:S(2)}) copy-start(s32[32]{0:T(128)} %get-tuple-element.168) | copy-start | bytes 388
  931.2 16.8 %collective-permute-start.2 = (f32[5,1,16,128]{3,2,1,0:T(8,128)S(1)}, f32[5,1,16,128]{3,2,1,0:T(8,128)S(1)}, u32[]{:S(2)}, u32[]{:S(2)}) collective-permute-start(f32[5,1,16,128]{3,2,1,0:T(8,128)S(1)} %get-tuple-element.142), channel_id=1, source_target_pairs={{0,8},{8,16},{16,24},{1,9},{9,17},{17,25},{2,10},{10,18},{18,26},{... | collective-permute-start | bytes 122888 | tf_op jit(solution)/shard_map/ppermute | solution.py:23
  942.3 5.8 collective-permute-start.3
  948.2 4.5 collective-permute-start.4
  950.7 6.3 collective-permute-start.5
  (26 other events, 33.8 us)
Sparse Core Ops, SparseCore 0:
  55.3 217.1 all-gather.2
  274.5 84.9 all-gather.4
  930.3 110.4 reduce-scatter.1
where the time goes:
time: 1060 us; the launch traced here: 1050 us
  local copies, waits for them, and re-layouts  561 us (53%)
  waiting for transfers between devices  253 us (24%)
  other arithmetic  155 us (15%)
  matrix products  47.3 us (4%)
  starting transfers between devices  19.4 us (2%)
  between operations  15.5 us (1%)
    all_gather x1, waiting for transfers between devices, local(): slab_faces = lax.all_gather(own_faces, 'patch', axis=2, tiled=True)  146 us
    unnamed x179, local copies, waits for them, and re-layouts  124 us
    reduce_scatter x1, waiting for transfers between devices, local(): contrib = lax.psum_scatter(placed, 'patch', scatter_dimension=2, tiled=True)  82.4 us
    slice x1, local copies, waits for them, and re-layouts, coarse_faces(): blocks[:, :, :, :, H - 1]  56.7 us
    reshape x2, local copies, waits for them, and re-layouts, block_form(): slab.reshape(5, layer_depth, H, GZ + 2, H, GY + 2, H)  53.2 us
    reduce_sum x1, other arithmetic, cell_mean(): return fields.reshape(extents[0], extents[1], extents[2] // 2, 2, extents...  49.4 us
    sub x1, local copies, waits for them, and re-layouts, advance(): updated = fields - fine_rate * change  34.2 us
    transpose x1, local copies, waits for them, and re-layouts, slab_form(): blocks.reshape(5, layer_depth, H, H, H, GZ + 2, GY + 2)  29.1 us
  transfers between devices with their start and end apart: 9, of which 5 were waited for; matrix products, arithmetic and copies ran while one was open for 13% of the time, Pallas kernels for 0%

commit v1 on v0

--- a/solution.py
+++ b/solution.py
@@ -1,7 +1,9 @@
+import functools
 import jax
 import jax.numpy as jnp
 from jax import lax
 from jax.sharding import PartitionSpec as P
+from jax.lax import all_to_all, axis_size
 
 P_SIZE = 32
 LX = 1
@@ -13,6 +15,16 @@
 fine_rate = 0.1
 coarse_rate = 0.05
 highest = lax.Precision.HIGHEST
+
+
+def solve_the_panels(raw, ax_name):
+    return jnp.concatenate(
+        all_to_all(jnp.stack(tuple((raw for _ in range(axis_size(ax_name))))), ax_name, 0, 0),
+        axis=2,
+    )
+
+
+fill_lines_on_mesh = functools.partial(solve_the_panels, ax_name="patch")
 
 
 def padded(block, sides, width):
@@ -241,7 +253,7 @@
             cube_fields[..., P_SIZE - 1],
         ]
     )
-    slab_faces = lax.all_gather(own_faces, "patch", axis=2, tiled=True)
+    slab_faces = fill_lines_on_mesh(own_faces)
     slab_faces = jnp.take(slab_faces, inverse, axis=2)
     edge_faces = jnp.stack([slab_faces[0, :, :PYZ], slab_faces[1, :, -PYZ:]])
     rim_faces = padded(edge_faces, (("slab", 0),), 1)

time: 1060 us -> 1020 us (0.962)
  waiting for transfers between devices: 253 us -> 130 us
  local copies, waits for them, and re-layouts: 561 us -> 606 us
  starting transfers between devices: 19.4 us -> 46 us
    all_gather x1 -> x0, waiting for transfers between devices: 146 us -> none  [local(): slab_faces = lax.all_gather(own_faces, 'patch', axis=2, tiled=True)]
    all_to_all x0 -> x1, waiting for transfers between devices: none -> 42.2 us  [solve_the_panels(): all_to_all(jnp.stack(tuple((raw for _ in range(axis_size(ax_name))))), ax...]
    ppermute x3, starting transfers between devices: 15 us -> 34 us  [padded(): lax.ppermute(lax.slice_in_dim(block, block.shape[dim] - width, None, axis...]
    all_gather x1, waiting for transfers between devices: 18 us -> 0.01 us  [local(): whole_slab = lax.all_gather(coarse, 'patch', axis=2, tiled=True)]
    all_to_all x0 -> x2, local copies, waits for them, and re-layouts: none -> 15.2 us  [solve_the_panels(): all_to_all(jnp.stack(tuple((raw for _ in range(axis_size(ax_name))))), ax...]
    all_to_all x0 -> x1, other arithmetic: none -> 13 us  [solve_the_panels(): all_to_all(jnp.stack(tuple((raw for _ in range(axis_size(ax_name))))), ax...]
    unnamed x179 -> x212, local copies, waits for them, and re-layouts: 124 us -> 130 us
    unnamed x42 -> x43, other arithmetic: 26.1 us -> 26.2 us
  transfers between devices with their start and end apart: 9 -> 9, of which waited for: 5 -> 4; matrix products, arithmetic and copies ran while one was open for 13% -> 24% of each run, Pallas kernels for 0% -> 0%
where the time goes in v1:
time: 1020 us; the launch traced here: 1010 us
  local copies, waits for them, and re-layouts  606 us (59%)
  other arithmetic  163 us (16%)
  waiting for transfers between devices  130 us (13%)
  matrix products  47.2 us (5%)
  starting transfers between devices  46 us (5%)
  between operations  16 us (2%)
    unnamed x212, local copies, waits for them, and re-layouts  130 us
    reduce_scatter x1, waiting for transfers between devices, local(): contrib = lax.psum_scatter(placed, 'patch', scatter_dimension=2, tiled=True)  81.5 us
    slice x1, local copies, waits for them, and re-layouts, coarse_faces(): blocks[:, :, :, :, H - 1]  56.7 us
    reshape x2, local copies, waits for them, and re-layouts, block_form(): slab.reshape(5, layer_depth, H, GZ + 2, H, GY + 2, H)  53.2 us
    reduce_sum x1, other arithmetic, cell_mean(): return fields.reshape(extents[0], extents[1], extents[2] // 2, 2, extents...  49.4 us
    all_to_all x1, waiting for transfers between devices, solve_the_panels(): all_to_all(jnp.stack(tuple((raw for _ in range(axis_size(ax_name))))), ax...  42.2 us
    ppermute x3, starting transfers between devices, padded(): lax.ppermute(lax.slice_in_dim(block, block.shape[dim] - width, None, axis...  34 us
    sub x1, local copies, waits for them, and re-layouts, advance(): updated = fields - fine_rate * change  34 us
  transfers between devices with their start and end apart: 9, of which 4 were waited for; matrix products, arithmetic and copies ran while one was open for 24% of the time, Pallas kernels for 0%

profile of v1, /device:TPU:0, one launch (start us, length us, event | category | flops | bytes accessed | tf_op | source)
XLA Modules:
  0.0 1009.3 jit_solution(10271743467268553345)
XLA Ops:
  7.9 7.9 reshape.651
  17.0 3.1 fusion.227
  20.1 16.7 %fusion.226 = (f32[5,4,32,32,1]{4,3,2,1,0:T(8,128)}, f32[5,4,32,32,1]{4,3,2,1,0:T(8,128)}) fusion(f32[5,4,32,32,32]{4,3,2,1,0:T(8,128)} %reshape.651), kind=kLoop, calls=%fused_computation.626 | loop fusion | bytes 327680 | tf_op jit(solution)/shard_map/slice | solution.py:253
  36.8 6.7 copy.464
  43.5 7.5 copy.454
  52.1 7.5 stack.37
  59.6 12.3 %reshape.870 = f32[8,1,122880]{2,1,0:T(1,128)} reshape(f32[8,6,5,4,32,32]{5,4,3,2,1,0:T(8,128)} %stack.37) | data formatting | bytes 7864320
  71.9 7.6 all-to-all-start
  89.5 9.1 fusion.224
  109.9 6.1 slice.909
  121.7 5.0 copy.459
  140.0 42.2 %all-to-all-done = f32[8,1,122880]{2,1,0:T(1,128)} async-done(((f32[8,1,122880]{2,1,0:T(1,128)}), f32[8,1,122880]{2,1,0:T(1,128)}, u32[]{:S(2)}, u32[]{:S(2)}) %all-to-all-start) | async-done | bytes 3932192 | tf_op jit(solution)/shard_map/all_to_all | solution.py:22
  182.7 13.0 %reduce.6 = f32[8,122880]{1,0:T(8,128)} reduce(f32[8,1,122880]{2,1,0:T(1,128)} %all-to-all-done, f32[]{:T(128)} %broadcast.1234), dimensions={1}, to_apply=%all_to_all.3.reduce_sub_computation | reduce | bytes 7864324 | tf_op jit(solution)/shard_map/all_to_all | solution.py:22
  195.6 12.6 %reshape.871 = f32[8,6,5,4,32,32]{5,4,3,2,1,0:T(8,128)} reshape(f32[8,122880]{1,0:T(8,128)} %reduce.6) | data formatting | bytes 7864320
  208.3 14.7 %copy.371 = f32[8,6,5,4,32,32]{5,4,3,0,2,1:T(8,128)} copy(f32[8,6,5,4,32,32]{5,4,3,2,1,0:T(8,128)} %reshape.871) | data formatting | bytes 7864320 | tf_op jit(solution)/shard_map/all_to_all | solution.py:22
  223.0 13.4 %gather_fusion.2 = f32[32,6,5,32,32]{4,3,2,1,0:T(8,128)} fusion(f32[6,5,32,32,32]{4,3,2,1,0:T(8,128)} %bitcast.569, s32[1024]{0:T(1024)S(1)} %get-tuple-element.192), kind=kCustom, calls=%fused_computation.8 | custom fusion | bytes 7864448 | tf_op jit(solution)/shard_map/jit(_take)/gather | solution.py:257
  236.4 7.0 select_bitcast_fusion
  254.0 7.2 select_bitcast_fusion.2
  261.2 3.7 copy.378
  277.4 3.0 gather_fusion.15
  280.5 3.0 gather_fusion.16
  290.5 3.0 gather_fusion.18
  293.5 3.0 gather_fusion.20
  301.4 24.0 %reshape.656 = f32[5,1,16,8,16,8,16]{6,5,4,3,2,0,1:T(8,128)} reshape(f32[5,16,128,128]{3,2,1,0:T(8,128)} %all-gather.2.cloned.1.call-done) | data formatting | bytes 10485760 | tf_op jit(solution)/shard_map/reshape | solution.py:176
  325.4 29.2 %copy.514 = f32[5,1,16,8,16,8,16]{6,5,3,4,2,0,1:T(8,128)} copy(f32[5,1,16,8,16,8,16]{6,5,4,3,2,0,1:T(8,128)} %reshape.656) | data formatting | bytes 10485760 | tf_op jit(solution)/shard_map/reshape | solution.py:176
  354.5 56.7 %fusion.222 = (f32[5,1,16,16,1,64]{4,5,3,2,0,1:T(8,128)}, f32[5,1,16,16,1,64]{4,5,3,2,0,1:T(8,128)}) fusion(f32[5,1,16,16,16,64]{4,5,3,2,0,1:T(8,128)} %bitcast.565), kind=kLoop, calls=%fused_computation.622 | loop fusion | bytes 1310720 | tf_op jit(solution)/shard_map/slice | solution.py:206
  411.3 3.1 fusion.21
  419.5 23.0 %copy.480 = f32[5,1,16,16,1,64]{5,3,2,0,4,1:T(8,128)S(1)} copy(f32[5,1,16,16,1,64]{4,5,3,2,0,1:T(8,128)} %get-tuple-element.57) | data formatting | bytes 655360
  442.6 4.7 convolution_bitcast_fusion.4
  452.4 3.1 fusion.20
  456.4 4.6 tile.8
  461.0 9.0 tile.9
  470.0 22.6 %copy.479 = f32[5,1,16,16,1,64]{5,3,2,0,4,1:T(8,128)S(1)} copy(f32[5,1,16,16,1,64]{4,5,3,2,0,1:T(8,128)} %get-tuple-element.58) | data formatting | bytes 655360
  492.7 4.7 convolution_bitcast_fusion.5
  498.2 5.8 broadcast_in_dim.211
  504.1 9.3 reshape.667
  530.7 11.9 %constant_dynamic-update-slice_fusion.1 = (f32[5,4,33,1024]{3,2,1,0:T(8,128)}, f32[5,4,32,1024]{3,2,1,0:T(8,128)}, f32[5,4,32,1024]{3,2,1,0:T(8,128)}) fusion(f32[5,4,32,1024]{3,2,1,0:T(8,128)S(1)} %copy-done.2, f32[5,4,32,1024]{3,2,1,0:T(8,128)} %copy-done.6, f32[4,32,1024]{2,1,0:T(8,128)S(1)} %get-tuple-element.89, ...), kind=kLoop, calls=%fused_computation.345 | loop fusion | flops 6553599 | bytes 27262976
  542.6 8.1 reshape.673
  556.0 3.3 reduce_sum.257
  563.6 3.3 reduce_sum.256
  569.7 10.6 %slice.916 = f32[5,4,32,32,1]{4,3,2,1,0:T(8,128)} slice(f32[5,4,32,32,32]{4,3,2,1,0:T(8,128)} %reshape.673), slice={[0:5], [0:4], [0:32], [0:32], [31:32]} | slice | bytes 163840 | tf_op jit(solution)/shard_map/slice | solution.py:117
  580.4 27.1 %copy.483 = f32[5,4,32,32,1]{0,3,2,1,4:T(8,128)} copy(f32[5,4,32,32,1]{4,3,2,1,0:T(8,128)} %slice.916) | data formatting | bytes 163840
  607.5 3.3 reduce_sum.255
  613.6 3.3 reduce_sum.254
  619.7 3.1 dynamic-update-slice.79
  630.8 4.7 tile.20
  635.5 9.0 tile.21
  644.5 5.8 broadcast_in_dim.216
  650.3 9.1 reshape.671
  659.4 3.9 multiply_bitcast_fusion
  663.4 4.7 fusion.5
  669.4 3.9 fusion.11
  673.3 34.0 %copy.431 = f32[5,4,32,1024]{0,3,2,1:T(8,128)} copy(f32[5,4,32,1024]{3,2,1,0:T(8,128)} %fusion.11) | data formatting | bytes 5242880 | tf_op jit(solution)/shard_map/sub | solution.py:116
  707.3 49.4 %reduce_sum.253 = f32[5,4,16,16,16]{0,4,3,2,1:T(8,128)} reduce(f32[5,4,16,2,16,2,16,2]{0,7,6,5,4,3,2,1:T(2,128)} %bitcast.106, f32[]{:T(128)} %constant.88.clone.1), dimensions={3,5,7}, to_apply=%region_19.21 | reduce | flops 573440 | bytes 2949124 | tf_op jit(solution)/shard_map/reduce_sum | solution.py:135
  756.7 9.3 copy.432
  767.8 23.2 %fusion.2 = f32[5,1,16,16,16,64]{5,4,3,2,0,1:T(8,128)} fusion(f32[16]{0:T(128)S(1)} %copy-done.94, f32[5,16,16,64]{3,2,1,0:T(8,128)S(1)} %copy-done.53, f32[16]{0:T(128)S(1)} %copy-done.95, f32[5,16,16,64]{3,2,1,0:T(8,128)S(1)} %copy-done.54, f32[5,16,16,64]{3,2,1,0:T(8,128)S(1)} %copy-done.55, f32[5,16,16,64]{3,2,1,0:T(8,128)S(1)} %copy-done.56, ...), kind=kOutput, calls=%fused_computation.33 | convolution fusion | flops 73400832 | bytes 6881440 | tf_op jit(solution)/shard_map/nl,nb,vnxzy->vlxzyb/dot_general | solution.py:226
  790.9 24.3 %copy.446 = f32[5,1,16,16,16,64]{4,5,3,2,0,1:T(8,128)} copy(f32[5,1,16,16,16,64]{5,4,3,2,0,1:T(8,128)} %fusion.2) | data formatting | bytes 10485760 | tf_op jit(solution)/shard_map/add | solution.py:232
  815.3 29.1 %copy.447 = f32[5,1,16,8,16,8,16]{6,5,4,3,2,0,1:T(8,128)} copy(f32[5,1,16,8,16,8,16]{6,5,3,4,2,0,1:T(8,128)} %bitcast.568) | data formatting | bytes 10485760 | tf_op jit(solution)/shard_map/transpose | solution.py:182
  844.4 26.5 %reshape.677 = f32[5,16,128,128]{3,2,1,0:T(8,128)} reshape(f32[5,1,16,8,16,8,16]{6,5,4,3,2,0,1:T(8,128)} %copy.447) | data formatting | bytes 10485760 | tf_op jit(solution)/shard_map/reshape | solution.py:183
  871.9 28.9 %collective-permute-start.2 = (f32[5,1,16,128]{3,2,1,0:T(8,128)S(1)}, f32[5,1,16,128]{3,2,1,0:T(8,128)S(1)}, u32[]{:S(2)}, u32[]{:S(2)}) collective-permute-start(f32[5,1,16,128]{3,2,1,0:T(8,128)S(1)} %get-tuple-element.145), channel_id=1, source_target_pairs={{0,8},{8,16},{16,24},{1,9},{9,17},{17,25},{2,10},{10,18},{18,26},{... | collective-permute-start | bytes 122888 | tf_op jit(solution)/shard_map/ppermute | solution.py:35
  906.8 3.4 collective-permute-start.4
  912.2 4.3 collective-permute-done.5
  917.8 81.5 %reduce-scatter.2.cloned.1.call-done = f32[5,16,16,128]{3,2,1,0:T(8,128)} async-done(((f32[5,16,128,128]{3,2,1,0:T(8,128)}), f32[5,16,16,128]{3,2,1,0:T(8,128)}) %reduce-scatter.2.cloned.1.call-update) | async-done | bytes 655376 | tf_op jit(solution)/shard_map/reduce_scatter | solution.py:302
  999.4 2.9 add_select_fusion
  (424 shorter events, 145.8 us)
Async XLA Ops:
  7.2 294.2 %all-gather.2.cloned.1.call-start = ((), (), s32[]{:S(2)}) async-start(), calls=%async_computation.2 | async-start | bytes 5898240 | tf_op jit(solution)/shard_map/all_gather | solution.py:270
  20.1 30.9 %copy-start.33 = (f32[5,4,32,1,32]{4,3,2,1,0:T(1,128)}, f32[5,4,32,1,32]{4,3,2,1,0:T(1,128)S(1)}, u32[]{:S(2)}) copy-start(f32[5,4,32,1,32]{4,3,2,1,0:T(1,128)S(1)} %get-tuple-element.80) | copy-start | bytes 245764
  43.5 7.6 copy-start.37
  71.9 8.7 copy-start
  71.9 9.3 copy-start.81
  71.9 110.3 %all-to-all-start = ((f32[8,1,122880]{2,1,0:T(1,128)}), f32[8,1,122880]{2,1,0:T(1,128)}, u32[]{:S(2)}, u32[]{:S(2)}) async-start(f32[8,1,122880]{2,1,0:T(1,128)} %reshape.870), calls=%async_computation | async-start | bytes 7864320 | tf_op jit(solution)/shard_map/all_to_all | solution.py:22
  79.5 919.9 %reduce-scatter.2.cloned.1.call-start = ((), (), s32[]{:S(2)}) async-start(), calls=%async_computation.3 | async-start | bytes 5898240 | tf_op jit(solution)/shard_map/reduce_scatter | solution.py:302
  88.5 44.7 %copy-start.59 = (f32[1,4,32,1,32]{4,3,2,1,0:T(1,128)}, f32[1,4,32,1,32]{4,3,2,1,0:T(1,128)S(1)}, u32[]{:S(2)}) copy-start(f32[1,4,32,1,32]{4,3,2,1,0:T(1,128)S(1)} %get-tuple-element.76) | copy-start | bytes 49156
  88.5 49.6 %copy-start.49 = (f32[1,4,32,1,32]{4,3,2,1,0:T(1,128)}, f32[1,4,32,1,32]{4,3,2,1,0:T(1,128)S(1)}, u32[]{:S(2)}) copy-start(f32[1,4,32,1,32]{4,3,2,1,0:T(1,128)S(1)} %get-tuple-element.72) | copy-start | bytes 49156
  89.5 11.0 %copy-start.1 = (f32[5,4,32,1024]{3,2,1,0:T(8,128)S(1)}, f32[5,4,32,1024]{3,2,1,0:T(8,128)}, u32[]{:S(2)}) copy-start(f32[5,4,32,1024]{3,2,1,0:T(8,128)} %param.7) | copy-start | bytes 7864324
  98.7 38.7 %copy-start.57 = (f32[4,32,32]{2,1,0:T(8,128)}, f32[4,32,32]{2,1,0:T(8,128)S(1)}, u32[]{:S(2)}) copy-start(f32[4,32,32]{2,1,0:T(8,128)S(1)} %get-tuple-element.69) | copy-start | bytes 49156
  121.7 14.6 %copy-start.61 = (f32[1,4,32,32,1]{3,2,1,4,0:T(8,128)}, f32[1,4,32,32,1]{3,2,1,4,0:T(8,128)S(1)}, u32[]{:S(2)}) copy-start(f32[1,4,32,32,1]{3,2,1,4,0:T(8,128)S(1)} %copy.482) | copy-start | bytes 49156
  130.3 9.7 copy-start.70
  133.2 4.9 copy-start.41
  133.3 4.9 copy-start.51
  136.4 59.3 %copy-start.63 = (f32[4,32,32]{2,1,0:T(8,128)}, f32[4,32,32]{2,1,0:T(8,128)S(1)}, u32[]{:S(2)}) copy-start(f32[4,32,32]{2,1,0:T(8,128)S(1)} %get-tuple-element.159) | copy-start | bytes 49156
  244.0 6.7 collective-permute-start
  245.7 8.3 collective-permute-start.1
  261.2 3.7 copy-start.21
  285.8 14.6 %copy-start.27 = (f32[5,4,1,1024]{3,2,1,0:T(1,128)}, f32[5,4,1,1024]{3,2,1,0:T(1,128)S(1)}, u32[]{:S(2)}) copy-start(f32[5,4,1,1024]{3,2,1,0:T(1,128)S(1)} %copy.374) | copy-start | bytes 245764
  354.5 56.7 %copy-start.69 = (f32[4]{0:T(128)S(1)}, f32[4]{0:T(128)}, u32[]{:S(2)}) copy-start(f32[4]{0:T(128)} %get-tuple-element.186) | copy-start | bytes 52
  354.5 56.7 %copy-start.72 = (s32[4]{0:T(128)S(1)}, s32[4]{0:T(128)}, u32[]{:S(2)}) copy-start(s32[4]{0:T(128)} %get-tuple-element.173) | copy-start | bytes 52
  411.3 3.9 copy-start.43
  411.3 3.9 copy-start.80
  411.3 3.9 copy-start.85
  419.5 23.1 %copy-start.71 = (s32[4]{0:T(128)S(1)}, s32[4]{0:T(128)}, u32[]{:S(2)}) copy-start(s32[4]{0:T(128)} %copy-done.70) | copy-start | bytes 52
  442.6 5.4 copy-start.42
  442.6 5.4 copy-start.79
  442.6 5.4 copy-start.84
  448.4 4.1 copy-start.73
  452.4 3.8 copy-start.78
  452.4 3.8 copy-start.83
  470.0 22.7 %copy-start.76 = (s32[4]{0:T(128)S(1)}, s32[4]{0:T(128)}, u32[]{:S(2)}) copy-start(s32[4]{0:T(128)} %broadcast_add_fusion) | copy-start | bytes 52
  492.7 5.4 copy-start.77
  492.7 5.4 copy-start.82
  504.1 9.3 slice-start.1
  504.1 9.3 copy-start.15
  504.1 9.4 copy-start.87
  516.3 3.4 copy-start.11
  516.3 3.5 copy-start.40
  521.6 3.6 copy-start.31
  553.7 6.8 copy-start.35
  553.7 6.8 copy-start.91
  559.3 8.2 copy-start.90
  607.5 3.9 copy-start.89
  610.8 6.7 copy-start.88
  611.5 8.2 copy-start.68
  635.5 9.0 copy-start.45
  650.3 9.1 copy-start.25
  650.3 9.1 copy-start.28
  659.4 4.0 copy-start.5
  663.4 4.8 copy-start.8
  663.4 4.8 copy-start.9
  663.4 5.2 copy-start.22
  663.4 6.0 copy-start.23
  663.4 6.0 copy-start.36
  663.4 6.0 copy-start.46
  663.4 6.0 copy-start.74
  663.4 6.0 copy-start.75
  870.8 31.3 %copy-start.92 = (s32[32]{0:T(128)S(1)}, s32[32]{0:T(128)}, u32[]{:S(2)}) copy-start(s32[32]{0:T(128)} %get-tuple-element.166) | copy-start | bytes 388
  871.9 34.7 %collective-permute-start.2 = (f32[5,1,16,128]{3,2,1,0:T(8,128)S(1)}, f32[5,1,16,128]{3,2,1,0:T(8,128)S(1)}, u32[]{:S(2)}, u32[]{:S(2)}) collective-permute-start(f32[5,1,16,128]{3,2,1,0:T(8,128)S(1)} %get-tuple-element.145), channel_id=1, source_target_pairs={{0,8},{8,16},{16,24},{1,9},{9,17},{17,25},{2,10},{10,18},{18,26},{... | collective-permute-start | bytes 122888 | tf_op jit(solution)/shard_map/ppermute | solution.py:35
  900.9 5.8 collective-permute-start.3
  906.8 5.4 collective-permute-start.4
  910.2 6.3 collective-permute-start.5
  (43 other events, 77.1 us)
Sparse Core Ops, SparseCore 0:
  10.0 102.6 all-gather.1
  871.0 128.3 reduce-scatter.1
